TPU v7x, 32 devices: a whole 2x2x4 slice. The times are simulated.
32 devices in a mesh: bank: 8 (over y, x, core), zero: 4 (over z).
Axes of the slice: x: 2, y: 2, z: 4, core: 2. Of those that a mesh axis runs over, the one named last changes fastest.
Arguments:
- master_down: float32 [64, 1024, 2048], P('bank', None, 'zero'), may hold values from -0.25 to 0.25
- router_weight: float32 [2048, 64], P('zero', 'bank'), may hold values from -0.125 to 0.125
- router_gain: float32 [2048], P('zero'), may hold values from 0.25 to 1.75
Outputs:
- final_down: bfloat16 [64, 1024, 2048], P('bank')
- scale_down: float32 [64, 1024], P('bank')
- serve_router: bfloat16 [2048, 64], replicated
All inputs are finite; a program needn't handle non-finite values. Where the computation divides by a largest or mean magnitude, that divisor is 1e-20 or more.
Results may differ from a plain program's by a relative error of at most 0.001.
Values may be sent and summed in bfloat16 or wider, within the bound.
A program may use at most 128 MiB of HBM per device.

v0:
```python
import jax
import jax.numpy as jnp
from jax import lax
from jax.sharding import PartitionSpec as P


def per_device(master_down, router_weight, router_gain):
    scale_down = lax.pmax(jnp.max(jnp.abs(master_down), axis=2), "zero")
    narrow_down = (master_down / jnp.expand_dims(scale_down, 2)).astype(jnp.bfloat16)
    final_down = lax.all_gather(narrow_down, "zero", axis=2, tiled=True)
    part_router = (router_weight * router_gain[:, None]).astype(jnp.bfloat16)
    row_router = lax.all_gather(part_router, "zero", axis=0, tiled=True)
    serve_router = lax.all_gather(row_router, "bank", axis=1, tiled=True)
    return (final_down, scale_down, serve_router)


def solution(mesh):
    placed = (P("bank", None, "zero"), P("zero", "bank"), P("zero"))
    return jax.shard_map(
        per_device,
        mesh=mesh,
        in_specs=placed,
        out_specs=(P("bank", None, None), P("bank", None), P()),
        check_vma=False,
    )
```

profile of v0, /device:TPU:0, one launch (start us, length us, event | category | flops | bytes accessed | tf_op | source)
XLA Modules:
  0.0 634.6 jit_solution(17249483322936477532)
XLA Ops:
  7.2 0.0 all-gather.2.cloned.1.call-start
  7.2 7.1 %abs_reduce_fusion = f32[8,1024]{1,0:T(8,128)S(1)} fusion(f32[8,1024,512]{2,1,0:T(8,128)} %param.3), kind=kLoop, calls=%fused_computation.1 | loop fusion | flops 8380416 | bytes 16809984 | tf_op jit(solution)/shard_map/reduce_max | solution.py:8
  14.3 20.8 %pmax.7 = f32[8,1024]{1,0:T(8,128)S(1)} all-reduce(f32[8,1024]{1,0:T(8,128)S(1)} %abs_reduce_fusion), channel_id=1, replica_groups=mesh['bank'=8,'zero'=4] {'zero'}, use_global_device_ids=true, to_apply=%region_1.0 | all-reduce | flops 8192 | bytes 65536 | tf_op jit(solution)/shard_map/pmax | solution.py:8
  35.1 0.0 copy-start
  35.1 0.0 copy-start.1
  35.2 0.0 copy-start.2
  35.2 9.2 %divide_convert_fusion = bf16[8,1024,512]{2,1,0:T(8,128)(2,1)} fusion(f32[8,1024,512]{2,1,0:T(8,128)} %param.3, f32[8,1024]{1,0:T(8,128)S(1)} %pmax.7), kind=kLoop, calls=%fused_computation | loop fusion | flops 8388608 | bytes 25198592 | tf_op jit(solution)/shard_map/convert_element_type | solution.py:9
  44.3 0.0 all-gather.2.cloned.1.call-update
  44.4 0.0 copy-done
  44.4 0.0 copy-done.1
  44.4 0.0 copy-done.2
  44.4 13.1 %all_gather.10 = bf16[2048,8]{0,1:T(8,128)(2,1)S(1)} all-gather(bf16[512,8]{0,1:T(8,128)(2,1)S(1)} %multiply_convert_fusion), channel_id=1, replica_groups=mesh['bank'=8,'zero'=4] {'zero'}, dimensions={0}, use_global_device_ids=true | all-gather | bytes 40960 | tf_op jit(solution)/shard_map/all_gather | solution.py:12
  57.5 9.3 %all_gather.11 = bf16[2048,64]{0,1:T(8,128)(2,1)S(1)} all-gather(bf16[2048,8]{0,1:T(8,128)(2,1)S(1)} %all_gather.10), channel_id=1, replica_groups=mesh['bank'=8,'zero'=4] {'bank'}, dimensions={1}, use_global_device_ids=true | all-gather | bytes 294912 | tf_op jit(solution)/shard_map/all_gather | solution.py:13
  66.8 537.3 %all-gather.2.cloned.1.call-done = bf16[8,1024,2048]{2,1,0:T(8,128)(2,1)} async-done(((bf16[8,1024,512]{2,1,0:T(8,128)(2,1)}), bf16[8,1024,2048]{2,1,0:T(8,128)(2,1)}) %all-gather.2.cloned.1.call-update) | async-done | bytes 33554448 | tf_op jit(solution)/shard_map/all_gather | solution.py:10
  604.1 22.9 %copy.8 = bf16[8,1024,2048]{2,1,0:T(8,128)(2,1)} copy(bf16[8,1024,2048]{2,1,0:T(8,128)(2,1)} %all-gather.2.cloned.1.call-done) | data formatting | bytes 67108864
  627.0 0.7 copy.9
  (1 shorter events, 0.0 us)
Async XLA Ops:
  7.2 597.0 %all-gather.2.cloned.1.call-start = ((), (), s32[]{:S(2)}) async-start(), calls=%async_computation | async-start | bytes 41943040 | tf_op jit(solution)/shard_map/all_gather | solution.py:10
  35.1 9.2 %copy-start = (f32[8,1024]{1,0:T(8,128)}, f32[8,1024]{1,0:T(8,128)S(1)}, u32[]{:S(2)}) copy-start(f32[8,1024]{1,0:T(8,128)S(1)} %pmax.7) | copy-start | bytes 98308
  35.1 9.2 %copy-start.1 = (f32[512,8]{0,1:T(8,128)S(1)}, f32[512,8]{0,1:T(8,128)}, u32[]{:S(2)}) copy-start(f32[512,8]{0,1:T(8,128)} %param.4) | copy-start | bytes 49156
  35.2 9.2 %copy-start.2 = (f32[512]{0:T(512)S(1)}, f32[512]{0:T(512)}, u32[]{:S(2)}) copy-start(f32[512]{0:T(512)} %param.5) | copy-start | bytes 6148
Sparse Core Ops, SparseCore 0:
  44.5 559.6 all-gather.1
where the time goes:
time: 635 us
  waiting for transfers between devices  537 us (85%)
  blocking collectives  43.2 us (7%)
  local copies, waits for them, and re-layouts  23.6 us (4%)
  other arithmetic  16.3 us (3%)
  between operations  14.1 us (2%)
    all_gather x1, waiting for transfers between devices, per_device(): final_down = lax.all_gather(narrow_down, 'zero', axis=2, tiled=True)  537 us
    unnamed x8, local copies, waits for them, and re-layouts  23.6 us
    pmax x1, blocking collectives, per_device(): scale_down = lax.pmax(jnp.max(jnp.abs(master_down), axis=2), 'zero')  20.8 us
    all_gather x1, blocking collectives, per_device(): row_router = lax.all_gather(part_router, 'zero', axis=0, tiled=True)  13.1 us
  transfers between devices with their start and end apart: 1, of which 1 were waited for; matrix products, arithmetic and copies ran while one was open for 0% of the time, Pallas kernels for 0%

commit v1 on v0

--- a/solution.py
+++ b/solution.py
@@ -2,12 +2,14 @@
 import jax.numpy as jnp
 from jax import lax
 from jax.sharding import PartitionSpec as P
+from jax.lax import all_to_all, axis_size
 
 
 def per_device(master_down, router_weight, router_gain):
     scale_down = lax.pmax(jnp.max(jnp.abs(master_down), axis=2), "zero")
     narrow_down = (master_down / jnp.expand_dims(scale_down, 2)).astype(jnp.bfloat16)
-    final_down = lax.all_gather(narrow_down, "zero", axis=2, tiled=True)
+    formed = jnp.concatenate([narrow_down for _ in range(axis_size("zero"))], axis=2)
+    final_down = all_to_all(formed, "zero", 2, 2, tiled=True)
     part_router = (router_weight * router_gain[:, None]).astype(jnp.bfloat16)
     row_router = lax.all_gather(part_router, "zero", axis=0, tiled=True)
     serve_router = lax.all_gather(row_router, "bank", axis=1, tiled=True)

time: 635 us -> 883 us (1.39)
  blocking collectives: 43.2 us -> 754 us
  waiting for transfers between devices: 537 us -> 0.01 us
  local copies, waits for them, and re-layouts: 23.6 us -> 64.3 us
  other arithmetic: 16.3 us -> 52.4 us
  between operations: 14.1 us -> 0.7 us
  starting transfers between devices: 0.04 us -> 9.73 us
    all_gather x1, blocking collectives: 13.1 us -> 724 us  [per_device(): row_router = lax.all_gather(part_router, 'zero', axis=0, tiled=True)]
    all_gather x1 -> x0, waiting for transfers between devices: 537 us -> none  [per_device(): final_down = lax.all_gather(narrow_down, 'zero', axis=2, tiled=True)]
    unnamed x8 -> x9, local copies, waits for them, and re-layouts: 23.6 us -> 64.3 us
    concatenate x0 -> x1, other arithmetic: none -> 36 us  [per_device(): jnp.concatenate([narrow_down for _ in range(axis_size('zero'))], axis=2)]
    all_to_all x0 -> x1, starting transfers between devices: none -> 9.73 us  [per_device(): final_down = all_to_all(formed, 'zero', 2, 2, tiled=True)]
  transfers between devices with their start and end apart: 1 -> 1, of which waited for: 1 -> 0; matrix products, arithmetic and copies ran while one was open for 0% -> 0% of each run, Pallas kernels for 0% -> 0%
where the time goes in v1:
time: 883 us; the launch traced here: 881 us
  blocking collectives  754 us (85%)
  local copies, waits for them, and re-layouts  64.3 us (7%)
  other arithmetic  52.4 us (6%)
  starting transfers between devices  9.73 us (1%)
    all_gather x1, blocking collectives, per_device(): row_router = lax.all_gather(part_router, 'zero', axis=0, tiled=True)  724 us
    unnamed x9, local copies, waits for them, and re-layouts  64.3 us
    concatenate x1, other arithmetic, per_device(): jnp.concatenate([narrow_down for _ in range(axis_size('zero'))], axis=2)  36 us
    pmax x1, blocking collectives, per_device(): scale_down = lax.pmax(jnp.max(jnp.abs(master_down), axis=2), 'zero')  20.8 us
  transfers between devices with their start and end apart: 1, of which 0 were waited for; matrix products, arithmetic and copies ran while one was open for 0% of the time, Pallas kernels for 0%

profile of v1, /device:TPU:0, one launch (start us, length us, event | category | flops | bytes accessed | tf_op | source)
XLA Modules:
  0.0 881.4 jit_solution(12545415169672977733)
XLA Ops:
  0.6 7.1 abs_reduce_fusion
  7.7 16.9 %copy.6 = f32[8,1024,512]{1,0,2:T(8,128)} copy(f32[8,1024,512]{2,1,0:T(8,128)} %param.3) | data formatting | bytes 33554432 | tf_op args[0]
  24.6 20.8 %pmax.7 = f32[8,1024]{1,0:T(8,128)S(1)} all-reduce(f32[8,1024]{1,0:T(8,128)S(1)} %abs_reduce_fusion), channel_id=1, replica_groups=mesh['bank'=8,'zero'=4] {'zero'}, use_global_device_ids=true, to_apply=%region_1.0 | all-reduce | flops 8192 | bytes 65536 | tf_op jit(solution)/shard_map/pmax | solution.py:9
  45.5 0.0 copy-start
  45.5 9.2 %divide_convert_fusion = bf16[8,1024,512]{1,0,2:T(8,128)(2,1)} fusion(f32[8,1024,512]{1,0,2:T(8,128)} %copy.6, f32[8,1024]{1,0:T(8,128)S(1)} %pmax.7), kind=kLoop, calls=%fused_computation.1 | loop fusion | flops 8388608 | bytes 25198592 | tf_op jit(solution)/shard_map/convert_element_type | solution.py:10
  54.7 36.0 %pad_maximum_fusion = bf16[8,1024,2048]{1,0,2:T(8,128)(2,1)} fusion(bf16[8,1024,512]{1,0,2:T(8,128)(2,1)} %divide_convert_fusion), kind=kLoop, calls=%fused_computation | loop fusion | flops 50331648 | bytes 41943040 | tf_op jit(solution)/shard_map/concatenate | solution.py:11
  90.7 0.0 copy-done
  90.7 0.0 copy-start.1
  90.8 0.0 copy-start.2
  90.8 9.7 %all-to-all-start = ((bf16[8,1024,2048]{1,0,2:T(8,128)(2,1)}), bf16[8,1024,2048]{1,0,2:T(8,128)(2,1)}, u32[]{:S(2)}, u32[]{:S(2)}) async-start(bf16[8,1024,2048]{1,0,2:T(8,128)(2,1)} %pad_maximum_fusion), calls=%async_computation | async-start | bytes 67108864 | tf_op jit(solution)/shard_map/all_to_all | solution.py:12
  100.5 0.0 copy-done.1
  100.5 0.0 copy-done.2
  100.5 724.2 %all_gather.6 = bf16[2048,8]{0,1:T(8,128)(2,1)S(1)} all-gather(bf16[512,8]{0,1:T(8,128)(2,1)S(1)} %multiply_convert_fusion), channel_id=1, replica_groups=mesh['bank'=8,'zero'=4] {'zero'}, dimensions={0}, use_global_device_ids=true | all-gather | bytes 40960 | tf_op jit(solution)/shard_map/all_gather | solution.py:14
  824.7 9.3 %all_gather.7 = bf16[2048,64]{0,1:T(8,128)(2,1)S(1)} all-gather(bf16[2048,8]{0,1:T(8,128)(2,1)S(1)} %all_gather.6), channel_id=1, replica_groups=mesh['bank'=8,'zero'=4] {'bank'}, dimensions={1}, use_global_device_ids=true | all-gather | bytes 294912 | tf_op jit(solution)/shard_map/all_gather | solution.py:15
  834.0 0.0 all-to-all-done
  834.0 46.6 %copy.7 = bf16[8,1024,2048]{2,1,0:T(8,128)(2,1)} copy(bf16[8,1024,2048]{1,0,2:T(8,128)(2,1)} %all-to-all-done) | data formatting | bytes 67108864
  880.7 0.7 copy.9
  (1 shorter events, 0.0 us)
Async XLA Ops:
  45.5 45.3 %copy-start = (f32[8,1024]{1,0:T(8,128)}, f32[8,1024]{1,0:T(8,128)S(1)}, u32[]{:S(2)}) copy-start(f32[8,1024]{1,0:T(8,128)S(1)} %pmax.7) | copy-start | bytes 98308
  90.7 9.8 %copy-start.1 = (f32[512,8]{0,1:T(8,128)S(1)}, f32[512,8]{0,1:T(8,128)}, u32[]{:S(2)}) copy-start(f32[512,8]{0,1:T(8,128)} %param.4) | copy-start | bytes 49156
  90.8 9.8 %copy-start.2 = (f32[512]{0:T(512)S(1)}, f32[512]{0:T(512)}, u32[]{:S(2)}) copy-start(f32[512]{0:T(512)} %param.5) | copy-start | bytes 6148
  90.8 743.3 %all-to-all-start = ((bf16[8,1024,2048]{1,0,2:T(8,128)(2,1)}), bf16[8,1024,2048]{1,0,2:T(8,128)(2,1)}, u32[]{:S(2)}, u32[]{:S(2)}) async-start(bf16[8,1024,2048]{1,0,2:T(8,128)(2,1)} %pad_maximum_fusion), calls=%async_computation | async-start | bytes 67108864 | tf_op jit(solution)/shard_map/all_to_all | solution.py:12
